TPU v7x, 32 devices: a whole 2x2x4 slice. The times are simulated.
32 devices in a mesh: groups: 2 (over y), seq: 4 (over z), batch: 2 (over x), head: 2 (over core).
Axes of the slice: x: 2, y: 2, z: 4, core: 2. Of those that a mesh axis runs over, the one named last changes fastest.
Arguments:
- hidden_in: bfloat16 [64, 4096], P(('groups', 'batch'), 'seq'), parts along dimension 0, may hold values from -400 to 400
- norm_gain_vector: bfloat16 [4096], P('seq'), may hold values from 0.099609375 to 1.8984375
- w_query: bfloat16 [4096, 4096], P('seq', 'head'), may hold values from -0.09375 to 0.09375
- key_cache_rows: bfloat16 [64, 4096, 128], P(('groups', 'batch'), 'seq'), parts along dimension 0, may hold values from -360 to 360
- value_cache_rows: bfloat16 [64, 4096, 128], P(('groups', 'batch'), 'seq'), parts along dimension 0, may hold values from -6 to 6
- k_new: bfloat16 [64, 128], P(('groups', 'batch')), parts along dimension 0, may hold values from -360 to 360
- v_new: bfloat16 [64, 128], P(('groups', 'batch')), parts along dimension 0, may hold values from -6 to 6
- lengths: int32 [64], P(('groups', 'batch')), parts along dimension 0, may hold values from 1 to 4096, as said below
- w_out: bfloat16 [4096, 4096], P('head', 'seq'), may hold values from -0.09375 to 0.09375
Outputs:
- layer_out: float32 [64, 4096], P(('groups', 'batch'), ('seq', 'head')), parts along dimension 0
There are 2 independent parts, one for each index of `groups`. A program takes and returns all parts, laid end to end along the dimension named above; an argument that names none is the same for every part. Nothing has to cross between parts.
Inputs may be any that keep to these rules, and one draw needn't show every extreme that they name: `lengths`: every sequence has at least one cached position; some sequence of each draw uses all 4096.
All inputs are finite; a program needn't handle non-finite values.
Results may differ from a plain program's by a relative error of at most 0.008.
Values sent between devices are 32-bit elements; how exact they have to be, the bound alone decides.
A program may use at most 64 MiB of HBM per device.

v0:
```python
import jax
import jax.numpy as jnp
from jax import lax
from jax.sharding import PartitionSpec as P

D = 4096
HD = 128


def combined_all(value, axis, join):
    pieces = jax.tree.map(lambda part: lax.all_gather(part, axis), value)
    head = jax.tree.map(lambda part: part[0], pieces)
    tail = jax.tree.map(lambda part: part[1:], pieces)
    total, _ = lax.scan(lambda total, share: (join(total, share), None), head, tail)
    return total


def combine(earlier, later):
    top_a, total_a, summed_a = earlier
    top_b, total_b, summed_b = later
    top = jnp.maximum(top_a, top_b)
    factor_a = jnp.exp(top_a - top)
    factor_b = jnp.exp(top_b - top)
    return (
        top,
        total_a * factor_a + total_b * factor_b,
        summed_a * factor_a[..., None] + summed_b * factor_b[..., None],
    )


def shards(
    hidden_in,
    norm_gain_vector,
    w_query,
    key_cache_rows,
    value_cache_rows,
    k_new,
    v_new,
    lengths,
    w_out,
):
    inputs = hidden_in.astype(jnp.float32)
    squares = lax.psum(jnp.sum(inputs * inputs, axis=-1), "seq")
    inv_rms = lax.rsqrt(squares / D + 1e-05)
    normed = (inputs * inv_rms[:, None] * norm_gain_vector.astype(jnp.float32)[None, :]).astype(
        jnp.bfloat16
    )
    partial_query = jnp.dot(normed, w_query, preferred_element_type=jnp.float32)
    inverse_root_norm = 1.0 / HD**0.5
    query_vectors = (lax.psum(partial_query, "seq") * inverse_root_norm).astype(jnp.bfloat16)
    seq_rows = query_vectors.shape[0]
    query_vectors = query_vectors.reshape(seq_rows, query_vectors.shape[1] // HD, HD)
    block_len = key_cache_rows.shape[1]
    scores = jnp.einsum(
        "irm,iam->ira", query_vectors, key_cache_rows, preferred_element_type=jnp.float32
    )
    own = jnp.einsum("bhd,bd->bh", query_vectors, k_new, preferred_element_type=jnp.float32)
    positions = lax.axis_index("seq") * block_len + lax.iota(jnp.int32, block_len)
    live_mask = (positions[None, :] < lengths[:, None])[:, None, :]
    local_top = jnp.maximum(jnp.max(jnp.where(live_mask, scores, -jnp.inf), axis=-1), own)
    softmax_weights = jnp.where(live_mask, jnp.exp(scores - local_top[..., None]), jnp.float32(0.0))
    local_total = jnp.sum(softmax_weights, axis=-1)
    local_partial_sum = jnp.einsum(
        "ajq,aqe->aje",
        softmax_weights.astype(jnp.bfloat16),
        value_cache_rows,
        preferred_element_type=jnp.float32,
    )
    top, totals, summed = combined_all((local_top, local_total, local_partial_sum), "seq", combine)
    fresh = jnp.exp(own - top)
    totals = totals + fresh
    result = (summed + fresh[..., None] * v_new.astype(jnp.float32)[:, None, :]) / totals[..., None]
    attended = result.astype(jnp.bfloat16).reshape(seq_rows, -1)
    partial_out = jnp.dot(attended, w_out, preferred_element_type=jnp.float32)
    return lax.psum_scatter(partial_out, "head", scatter_dimension=1, tiled=True)


def solution(mesh):
    placed = (
        P(("groups", "batch"), "seq"),
        P("seq"),
        P("seq", "head"),
        P(("groups", "batch"), "seq", None),
        P(("groups", "batch"), "seq", None),
        P(("groups", "batch"), None),
        P(("groups", "batch"), None),
        P(("groups", "batch")),
        P("head", "seq"),
    )
    return jax.shard_map(
        shards,
        mesh=mesh,
        in_specs=placed,
        out_specs=P(("groups", "batch"), ("seq", "head")),
        check_vma=False,
    )
```

profile of v0, /device:TPU:0, one launch (start us, length us, event | category | flops | bytes accessed | tf_op | source)
XLA Modules:
  0.0 123.9 jit_solution(10203687832632314913)
XLA Ops:
  6.5 0.0 copy-start
  6.5 0.0 copy-start.2
  6.5 0.0 copy-start.3
  6.5 0.0 all-reduce.2.cloned.1.call-start
  6.5 0.9 fusion.10
  7.5 13.5 %psum.14 = f32[16]{0:T(128)S(1)} all-reduce(f32[16]{0:T(128)S(1)} %fusion.10), channel_id=1, replica_groups=mesh['groups'=2,'seq'=4,'batch'=2,'head'=2] {'seq'}, use_global_device_ids=true, to_apply=%region_1.0 | all-reduce | flops 16 | bytes 128 | tf_op jit(solution)/shard_map/psum | solution.py:43
  20.9 0.7 convert_element_type.22
  21.6 3.6 %fusion.17 = f32[16,2048]{1,0:T(8,128)} fusion(bf16[1024,2048]{1,0:T(8,128)(2,1)} %param.13, bf16[16,1024]{1,0:T(8,128)(2,1)} %param.11, f32[1024]{0:T(1024)S(1)} %convert_element_type.22, f32[16]{0:T(128)S(1)} %add_rsqrt_fusion), kind=kOutput, calls=%fused_computation.27 | convolution fusion | flops 67174400 | bytes 4362304 | tf_op jit(solution)/shard_map/dot_general | solution.py:48
  25.2 0.0 all-reduce.2.cloned.1.call-update
  25.2 0.0 reduce-scatter.2.cloned.1.call-start
  25.3 0.0 copy-done.2
  25.3 0.0 copy-done.3
  25.3 0.1 broadcast_compare_fusion
  25.4 32.8 %all-reduce.2.cloned.1.call-done = f32[16,2048]{1,0:T(8,128)} async-done(((f32[16,2048]{1,0:T(8,128)}), f32[16,2048]{1,0:T(8,128)}) %all-reduce.2.cloned.1.call-update) | async-done | bytes 131088 | tf_op jit(solution)/shard_map/psum | solution.py:50
  58.3 1.1 fusion.13
  59.3 0.0 copy-done
  59.4 0.1 fusion.21
  59.5 3.5 %select_reduce_fusion = (f32[16,16]{1,0:T(8,128)S(1)}, f32[16,16,1024]{2,1,0:T(8,128)S(1)}) fusion(pred[16,1024]{1,0:T(8,128)(4,1)S(1)} %broadcast_compare_fusion, bf16[16,16,128]{2,1,0:T(8,128)(2,1)S(1)} %bitcast.42, bf16[16,1024,128]{2,1,0:T(8,128)(2,1)} %param.14), kind=kOutput, calls=%fused_computation.9 | convolution fusion | flops 67632896 | bytes 5325824 | tf_op jit(solution)/shard_map/irm,iam->ira/dot_general | solution.py:54
  63.0 13.1 %all-gather = f32[64,16]{1,0:T(8,128)S(1)} all-gather(f32[16,16]{1,0:T(8,128)S(1)} %max.6), channel_id=2, replica_groups=mesh['groups'=2,'seq'=4,'batch'=2,'head'=2] {'seq'}, dimensions={0}, use_global_device_ids=true | all-gather | bytes 5120 | tf_op jit(solution)/shard_map/all_gather | solution.py:11
  76.2 0.3 fusion.4
  76.5 13.2 %all-gather.1 = f32[64,16]{1,0:T(8,128)S(1)} all-gather(f32[16,16]{1,0:T(8,128)S(1)} %fusion.4), channel_id=3, replica_groups=mesh['groups'=2,'seq'=4,'batch'=2,'head'=2] {'seq'}, dimensions={0}, use_global_device_ids=true | all-gather | bytes 5120 | tf_op jit(solution)/shard_map/all_gather | solution.py:11
  89.8 0.0 copy-done.1
  89.8 0.8 fusion.5
  90.5 14.7 %all-gather.2 = f32[64,16,128]{2,1,0:T(8,128)S(1)} all-gather(f32[16,16,128]{2,1,0:T(8,128)S(1)} %fusion.5), channel_id=4, replica_groups=mesh['groups'=2,'seq'=4,'batch'=2,'head'=2] {'seq'}, dimensions={0}, use_global_device_ids=true | all-gather | bytes 655360 | tf_op jit(solution)/shard_map/all_gather | solution.py:11
  105.2 0.6 while.14
  105.3 0.2 fusion.35
  105.5 0.2 fusion.35
  105.7 0.2 fusion.35
  105.9 0.1 divide_convert_fusion
  106.0 3.5 %fusion.14 = f32[16,1024]{1,0:T(8,128)} fusion(bf16[2048,1024]{1,0:T(8,128)(2,1)} %param.19, bf16[2,8,16,128]{3,2,1,0:T(8,128)(2,1)S(1)} %bitcast.40), kind=kOutput, calls=%fused_computation.24 | convolution fusion | flops 67108864 | bytes 4325376 | tf_op jit(solution)/shard_map/dot_general | solution.py:74
  109.5 0.0 reduce-scatter.2.cloned.1.call-update
  109.5 7.6 %reduce-scatter.2.cloned.1.call-done = f32[16,512]{1,0:T(8,128)} async-done(((f32[16,1024]{1,0:T(8,128)}), f32[16,512]{1,0:T(8,128)}) %reduce-scatter.2.cloned.1.call-update) | async-done | bytes 32784 | tf_op jit(solution)/shard_map/reduce_scatter | solution.py:75
  (16 shorter events, 0.1 us)
Async XLA Ops:
  6.5 52.8 %copy-start = (bf16[16,128]{1,0:T(8,128)(2,1)S(1)}, bf16[16,128]{1,0:T(8,128)(2,1)}, u32[]{:S(2)}) copy-start(bf16[16,128]{1,0:T(8,128)(2,1)} %param.16) | copy-start | bytes 12292
  6.5 18.8 %copy-start.2 = (bf16[16,128]{1,0:T(8,128)(2,1)S(1)}, bf16[16,128]{1,0:T(8,128)(2,1)}, u32[]{:S(2)}) copy-start(bf16[16,128]{1,0:T(8,128)(2,1)} %param.17) | copy-start | bytes 12292
  6.5 18.8 %copy-start.3 = (s32[16]{0:T(128)S(1)}, s32[16]{0:T(128)}, u32[]{:S(2)}) copy-start(s32[16]{0:T(128)} %param.18) | copy-start | bytes 196
  6.5 51.7 %all-reduce.2.cloned.1.call-start = ((), (), s32[]{:S(2)}) async-start(), calls=%async_computation.1 | async-start | bytes 262144 | tf_op jit(solution)/shard_map/psum | solution.py:50
  25.2 91.8 %reduce-scatter.2.cloned.1.call-start = ((), (), s32[]{:S(2)}) async-start(), calls=%async_computation.2 | async-start | bytes 98304 | tf_op jit(solution)/shard_map/reduce_scatter | solution.py:75
  58.3 31.5 %copy-start.1 = (bf16[16,1024,128]{2,1,0:T(8,128)(2,1)S(1)}, bf16[16,1024,128]{2,1,0:T(8,128)(2,1)}, u32[]{:S(2)}) copy-start(bf16[16,1024,128]{2,1,0:T(8,128)(2,1)} %param.15) | copy-start | bytes 12582916
Sparse Core Ops, SparseCore 0:
  25.3 32.8 all-reduce.1
  109.6 7.3 reduce-scatter.1
where the time goes:
time: 124 us
  blocking collectives  54.5 us (44%)
  waiting for transfers between devices  40.4 us (33%)
  between operations  13.5 us (11%)
  matrix products  11.5 us (9%)
  other arithmetic  3.82 us (3%)
    all_gather x3, blocking collectives, combined_all(): pieces = jax.tree.map(lambda part: lax.all_gather(part, axis), value)  41 us
    psum x1, waiting for transfers between devices, shards(): lax.psum(partial_query, 'seq') * inverse_root_norm  32.8 us
    psum x1, blocking collectives, shards(): squares = lax.psum(jnp.sum(inputs * inputs, axis=-1), 'seq')  13.5 us
    reduce_scatter x1, waiting for transfers between devices, shards(): lax.psum_scatter(partial_out, 'head', scatter_dimension=1, tiled=True)  7.55 us
    dot_general x1, matrix products, shards(): partial_query = jnp.dot(normed, w_query, preferred_element_type=jnp.float32)  3.56 us
    dot_general x1, matrix products, shards(): jnp.einsum('irm,iam->ira', query_vectors, key_cache_rows, preferred_eleme...  3.54 us
    dot_general x1, matrix products, shards(): partial_out = jnp.dot(attended, w_out, preferred_element_type=jnp.float32)  3.47 us
  transfers between devices with their start and end apart: 2, of which 2 were waited for; matrix products, arithmetic and copies ran while one was open for 0% of the time, Pallas kernels for 0%

commit v1 on v0

--- a/solution.py
+++ b/solution.py
@@ -5,6 +5,12 @@
 
 D = 4096
 HD = 128
+
+
+def gather_and_add(array, name):
+    shards = lax.all_gather(array, name, axis=0, tiled=False)
+    acc = shards.sum(axis=0)
+    return acc
 
 
 def combined_all(value, axis, join):
@@ -47,7 +53,7 @@
     )
     partial_query = jnp.dot(normed, w_query, preferred_element_type=jnp.float32)
     inverse_root_norm = 1.0 / HD**0.5
-    query_vectors = (lax.psum(partial_query, "seq") * inverse_root_norm).astype(jnp.bfloat16)
+    query_vectors = (gather_and_add(partial_query, "seq") * inverse_root_norm).astype(jnp.bfloat16)
     seq_rows = query_vectors.shape[0]
     query_vectors = query_vectors.reshape(seq_rows, query_vectors.shape[1] // HD, HD)
     block_len = key_cache_rows.shape[1]

time: 124 us -> 103 us (0.83)
  waiting for transfers between devices: 40.4 us -> 6.14 us
  blocking collectives: 54.5 us -> 69.5 us
    psum x1 -> x0, waiting for transfers between devices: 32.8 us -> none  [shards(): lax.psum(partial_query, 'seq') * inverse_root_norm]
    all_gather x0 -> x1, blocking collectives: none -> 14.8 us  [gather_and_add(): shards = lax.all_gather(array, name, axis=0, tiled=False)]
    reduce_scatter x1, waiting for transfers between devices: 7.55 us -> 6.13 us  [shards(): lax.psum_scatter(partial_out, 'head', scatter_dimension=1, tiled=True)]
  transfers between devices with their start and end apart: 2 -> 1, of which waited for: 2 -> 1; matrix products, arithmetic and copies ran while one was open for 0% -> 0% of each run, Pallas kernels for 0% -> 0%
where the time goes in v1:
time: 103 us
  blocking collectives  69.5 us (67%)
  between operations  13.5 us (13%)
  matrix products  10.9 us (11%)
  waiting for transfers between devices  6.14 us (6%)
  other arithmetic  2.79 us (3%)
    all_gather x3, blocking collectives, combined_all(): pieces = jax.tree.map(lambda part: lax.all_gather(part, axis), value)  41.3 us
    all_gather x1, blocking collectives, gather_and_add(): shards = lax.all_gather(array, name, axis=0, tiled=False)  14.8 us
    psum x1, blocking collectives, shards(): squares = lax.psum(jnp.sum(inputs * inputs, axis=-1), 'seq')  13.5 us
    reduce_scatter x1, waiting for transfers between devices, shards(): lax.psum_scatter(partial_out, 'head', scatter_dimension=1, tiled=True)  6.13 us
    dot_general x1, matrix products, shards(): jnp.einsum('irm,iam->ira', query_vectors, key_cache_rows, preferred_eleme...  3.63 us
    dot_general x1, matrix products, shards(): partial_out = jnp.dot(attended, w_out, preferred_element_type=jnp.float32)  3.47 us
    dot_general x1, matrix products, shards(): partial_query = jnp.dot(normed, w_query, preferred_element_type=jnp.float32)  2.9 us
  transfers between devices with their start and end apart: 1, of which 1 were waited for; matrix products, arithmetic and copies ran while one was open for 0% of the time, Pallas kernels for 0%

profile of v1, /device:TPU:0, one launch (start us, length us, event | category | flops | bytes accessed | tf_op | source)
XLA Modules:
  0.0 103.0 jit_solution(2800619958699315193)
XLA Ops:
  6.5 0.0 copy-start
  6.5 0.0 copy-start.3
  6.5 0.0 reduce-scatter.2.cloned.1.call-start
  6.5 0.9 fusion.10
  7.4 13.5 %psum.7 = f32[16]{0:T(128)S(1)} all-reduce(f32[16]{0:T(128)S(1)} %fusion.10), channel_id=1, replica_groups=mesh['groups'=2,'seq'=4,'batch'=2,'head'=2] {'seq'}, use_global_device_ids=true, to_apply=%region_1.0 | all-reduce | flops 16 | bytes 128 | tf_op jit(solution)/shard_map/psum | solution.py:49
  20.9 0.7 convert_element_type.26
  21.6 2.9 %fusion.17 = f32[16,2048]{1,0:T(8,128)S(1)} fusion(bf16[1024,2048]{1,0:T(8,128)(2,1)} %param.13, bf16[16,1024]{1,0:T(8,128)(2,1)} %param.11, f32[1024]{0:T(1024)S(1)} %convert_element_type.26, f32[16]{0:T(128)S(1)} %add_rsqrt_fusion), kind=kOutput, calls=%fused_computation.27 | convolution fusion | flops 67174400 | bytes 4362304 | tf_op jit(solution)/shard_map/dot_general | solution.py:54
  24.5 14.8 %all-gather = f32[64,2048]{1,0:T(8,128)S(1)} all-gather(f32[16,2048]{1,0:T(8,128)S(1)} %fusion.17), channel_id=2, replica_groups=mesh['groups'=2,'seq'=4,'batch'=2,'head'=2] {'seq'}, dimensions={0}, use_global_device_ids=true | all-gather | bytes 655360 | tf_op jit(solution)/shard_map/all_gather | solution.py:11
  39.3 0.0 copy-start.1
  39.4 0.0 copy-done.3
  39.4 0.1 broadcast_compare_fusion
  39.5 0.0 copy-done
  39.5 0.1 fusion.21
  39.6 3.6 %select_reduce_fusion = (f32[16,16]{1,0:T(8,128)S(1)}, f32[16,16,1024]{2,1,0:T(8,128)S(1)}) fusion(pred[16,1024]{1,0:T(8,128)(4,1)S(1)} %broadcast_compare_fusion, bf16[16,16,128]{2,1,0:T(8,128)(2,1)S(1)} %bitcast.44, bf16[16,1024,128]{2,1,0:T(8,128)(2,1)} %param.14), kind=kOutput, calls=%fused_computation.9 | convolution fusion | flops 67632896 | bytes 5325824 | tf_op jit(solution)/shard_map/irm,iam->ira/dot_general | solution.py:60
  43.3 0.0 copy-start.2
  43.3 13.3 %all-gather.1 = f32[64,16]{1,0:T(8,128)S(1)} all-gather(f32[16,16]{1,0:T(8,128)S(1)} %max.6), channel_id=3, replica_groups=mesh['groups'=2,'seq'=4,'batch'=2,'head'=2] {'seq'}, dimensions={0}, use_global_device_ids=true | all-gather | bytes 5120 | tf_op jit(solution)/shard_map/all_gather | solution.py:17
  56.6 0.3 fusion.4
  56.9 13.2 %all-gather.2 = f32[64,16]{1,0:T(8,128)S(1)} all-gather(f32[16,16]{1,0:T(8,128)S(1)} %fusion.4), channel_id=4, replica_groups=mesh['groups'=2,'seq'=4,'batch'=2,'head'=2] {'seq'}, dimensions={0}, use_global_device_ids=true | all-gather | bytes 5120 | tf_op jit(solution)/shard_map/all_gather | solution.py:17
  70.1 0.0 copy-done.1
  70.1 0.8 fusion.5
  70.9 14.8 %all-gather.3 = f32[64,16,128]{2,1,0:T(8,128)S(1)} all-gather(f32[16,16,128]{2,1,0:T(8,128)S(1)} %fusion.5), channel_id=5, replica_groups=mesh['groups'=2,'seq'=4,'batch'=2,'head'=2] {'seq'}, dimensions={0}, use_global_device_ids=true | all-gather | bytes 655360 | tf_op jit(solution)/shard_map/all_gather | solution.py:17
  85.7 0.0 copy-done.2
  85.7 0.6 while.14
  85.8 0.2 fusion.35
  86.0 0.2 fusion.35
  86.2 0.2 fusion.35
  86.4 0.1 divide_convert_fusion
  86.5 3.5 %fusion.14 = f32[16,1024]{1,0:T(8,128)} fusion(bf16[2048,1024]{1,0:T(8,128)(2,1)} %param.19, bf16[2,8,16,128]{3,2,1,0:T(8,128)(2,1)S(1)} %bitcast.42), kind=kOutput, calls=%fused_computation.24 | convolution fusion | flops 67108864 | bytes 4325376 | tf_op jit(solution)/shard_map/dot_general | solution.py:80
  90.0 0.0 reduce-scatter.2.cloned.1.call-update
  90.0 6.1 %reduce-scatter.2.cloned.1.call-done = f32[16,512]{1,0:T(8,128)} async-done(((f32[16,1024]{1,0:T(8,128)}), f32[16,512]{1,0:T(8,128)}) %reduce-scatter.2.cloned.1.call-update) | async-done | bytes 32784 | tf_op jit(solution)/shard_map/reduce_scatter | solution.py:81
  (17 shorter events, 0.2 us)
Async XLA Ops:
  6.5 32.9 %copy-start = (bf16[16,128]{1,0:T(8,128)(2,1)S(1)}, bf16[16,128]{1,0:T(8,128)(2,1)}, u32[]{:S(2)}) copy-start(bf16[16,128]{1,0:T(8,128)(2,1)} %param.16) | copy-start | bytes 12292
  6.5 32.8 %copy-start.3 = (s32[16]{0:T(128)S(1)}, s32[16]{0:T(128)}, u32[]{:S(2)}) copy-start(s32[16]{0:T(128)} %param.18) | copy-start | bytes 196
  6.5 89.6 %reduce-scatter.2.cloned.1.call-start = ((), (), s32[]{:S(2)}) async-start(), calls=%async_computation.1 | async-start | bytes 98304 | tf_op jit(solution)/shard_map/reduce_scatter | solution.py:81
  39.3 30.8 %copy-start.1 = (bf16[16,1024,128]{2,1,0:T(8,128)(2,1)S(1)}, bf16[16,1024,128]{2,1,0:T(8,128)(2,1)}, u32[]{:S(2)}) copy-start(bf16[16,1024,128]{2,1,0:T(8,128)(2,1)} %param.15) | copy-start | bytes 12582916
  43.3 42.5 %copy-start.2 = (bf16[16,128]{1,0:T(8,128)(2,1)S(1)}, bf16[16,128]{1,0:T(8,128)(2,1)}, u32[]{:S(2)}) copy-start(bf16[16,128]{1,0:T(8,128)(2,1)} %param.17) | copy-start | bytes 12292
Sparse Core Ops, SparseCore 0:
  90.2 5.9 reduce-scatter.1
